TPU v7x, 512 devices: a whole 4x4x16 slice. The times are simulated.
512 devices in a mesh: section: 8 (over x, y_hi), expert: 16 (over z), shard: 4 (over y_lo, core).
Axes of the slice: x: 4, y: 4 (y_hi: 2, y_lo: 2; y = y_hi * 2 + y_lo), z: 16, core: 2. Of those that a mesh axis runs over, the one named last changes fastest.
Arguments:
- fwd_in: bfloat16 [8, 2048, 3584], P('section', 'expert', 'shard'), may hold values from -6 to 6
- saved_in: bfloat16 [8, 2048, 3584], P('section', 'expert', 'shard'), may hold values from -6 to 6
- grad_in: bfloat16 [8, 2048, 3584], P('section', 'expert', 'shard'), may hold values from -6 to 6
- w_in: bfloat16 [8, 16, 3584, 1024], P('section', 'expert', 'shard'), may hold values from -0.09375 to 0.09375
- w_out: bfloat16 [8, 16, 1024, 3584], P('section', 'expert', None, 'shard'), may hold values from -0.1875 to 0.1875
- ids_fwd: int32 [8, 2048, 2], P('section', 'expert'), may hold values from 0 to 15, all different within a row; in each aligned block of 128 rows (0 to 127, 128 to 255, ..., all dimensions but the last counted through in order) at most 20 rows name the same one
- weight_fwd: int32 [8, 2048, 2], P('section', 'expert'), may hold values from 3277 to 65535
- ids_bwd: int32 [8, 2048, 2], P('section', 'expert'), may hold values from 0 to 15, all different within a row; in each aligned block of 128 rows (0 to 127, 128 to 255, ..., all dimensions but the last counted through in order) at most 20 rows name the same one
- weight_bwd: int32 [8, 2048, 2], P('section', 'expert'), may hold values from 3277 to 65535
Outputs:
- fwd_out: bfloat16 [8, 2048, 3584], P('section', 'expert', 'shard')
- bwd_out: bfloat16 [8, 2048, 3584], P('section', 'expert', 'shard')
Inputs may be any that keep to these rules, and one draw needn't show every extreme that they name: `ids_fwd`: the 2 experts of a token differ. In each layer, among the 128 tokens of one index of the expert axis, no expert is chosen by more than 20 slots. `ids_bwd`: the 2 experts of a token differ. In each layer, among the 128 tokens of one index of the expert axis, no expert is chosen by more than 20 slots.
All inputs are finite; a program needn't handle non-finite values.
Results may differ from a plain program's by a relative error of at most 0.0049.
Values may be sent and summed in bfloat16 or wider, within the bound.
No kernel may reach another device: no remote copies, remote signals or barrier semaphores. Data moves between devices by JAX's collectives and lax.ppermute only.
A program may use at most 64 MiB of HBM per device.

v0:
```python
import jax
import jax.numpy as jnp
from jax import lax
from jax.sharding import PartitionSpec as P


def sent_together(arrays, axis, split_dim, concat_dim, along):
    widths = [a.shape[along] for a in arrays]
    both = jnp.concatenate(arrays, axis=along)
    filled = lax.all_to_all(both, axis, split_axis=split_dim, concat_axis=concat_dim, tiled=True)
    return tuple(jnp.split(filled, [sum(widths[:k]) for k in range(1, len(widths))], axis=along))


def cut_along(array, dim, peers):
    lengths = array.shape
    tiles = array.reshape(*lengths[:dim], peers, lengths[dim] // peers, *lengths[dim + 1 :])
    return jnp.moveaxis(tiles, dim, 0)


def summed_on_arrival(array, axis, dim):
    tiles = cut_along(array, dim, lax.axis_size(axis))
    arrived = lax.all_to_all(tiles, axis, split_axis=0, concat_axis=0, tiled=True)
    return arrived.sum(axis=0)


def from_behind(value, axis, steps):
    count = lax.axis_size(axis)
    pairs = [(source, (source + steps) % count) for source in range(count)]
    return lax.ppermute(value, axis, pairs)


def in_one_piece(arrays, axis, dim, along):
    widths = [a.shape[along] for a in arrays]
    both = jnp.concatenate(arrays, axis=along)
    filled = summed_on_arrival(both, axis, dim)
    return tuple(jnp.split(filled, [sum(widths[:k]) for k in range(1, len(widths))], axis=along))


def destinations(route_ids, experts, capacity):
    tokens, slot_count = route_ids.shape
    flat_ids = route_ids.reshape(-1)
    labels = jnp.arange(experts, dtype=jnp.int32)
    onehot = (flat_ids[:, None] == labels[None, :]).astype(jnp.int32)
    before = jnp.cumsum(onehot, axis=0) - onehot
    ranking = jnp.sum(before * onehot, axis=1)
    return (flat_ids * capacity + ranking).reshape(tokens, slot_count)


def dispatch_matrix(targets, slot_total):
    labels = jnp.arange(slot_total, dtype=jnp.int32)
    hits = jnp.zeros((slot_total, targets.shape[0]), jnp.float32)
    for column in range(targets.shape[1]):
        hits = hits + (labels[:, None] == targets[None, :, column]).astype(jnp.float32)
    return hits.astype(jnp.bfloat16)


def by_expert(received, expert_group, local_experts, capacity):
    features = received.shape[-1]
    shaped = received.reshape(expert_group, local_experts, capacity, features)
    return shaped.transpose(1, 0, 2, 3).reshape(local_experts, expert_group * capacity, features)


def by_source(results, expert_group, local_experts, capacity):
    features = results.shape[-1]
    shaped = results.reshape(local_experts, expert_group, capacity, features)
    return shaped.transpose(1, 0, 2, 3).reshape(expert_group * local_experts * capacity, features)


def mix_rows(tok_rows, targets, route_weight, returned):
    picked = returned[targets].astype(jnp.float32)
    slot_weight = route_weight.astype(jnp.float32) / 32768.0
    summed = jnp.sum(slot_weight[:, :, None] * picked, axis=1)
    return (tok_rows.astype(jnp.float32) + summed).astype(jnp.bfloat16)


def per_device(fwd_in, saved_in, grad_in, w_in, w_out, ids_fwd, weight_fwd, ids_bwd, weight_bwd):
    expert_group = lax.axis_size("expert")
    local_experts = w_in.shape[1]
    experts = expert_group * local_experts
    tok_count = fwd_in.shape[1]
    slot_count = ids_fwd.shape[2]
    capacity = max(2, (tok_count * slot_count * 5 + 4 * experts - 1) // (4 * experts))
    slot_total = experts * capacity
    up_local = w_in[0]
    down_local = w_out[0]
    fwd_rows = fwd_in[0]
    saved_rows = saved_in[0]
    grad_rows = grad_in[0]
    fwd_targets = destinations(ids_fwd[0], experts, capacity)
    fwd_picker = dispatch_matrix(fwd_targets, slot_total)
    fwd_packed = jnp.dot(fwd_picker, fwd_rows, preferred_element_type=jnp.float32).astype(
        jnp.bfloat16
    )
    fwd_received = lax.all_to_all(fwd_packed, "expert", split_axis=0, concat_axis=0, tiled=True)
    fwd_slots = by_expert(fwd_received, expert_group, local_experts, capacity)
    bwd_targets = destinations(ids_bwd[0], experts, capacity)
    bwd_picker = dispatch_matrix(bwd_targets, slot_total)
    bwd_packed = jnp.dot(bwd_picker, saved_rows, preferred_element_type=jnp.float32).astype(
        jnp.bfloat16
    )
    grad_packed = jnp.dot(bwd_picker, grad_rows, preferred_element_type=jnp.float32).astype(
        jnp.bfloat16
    )
    bwd_received, grad_received = sent_together((bwd_packed, grad_packed), "expert", 0, 0, 1)
    bwd_slots = by_expert(bwd_received, expert_group, local_experts, capacity)
    grad_slots = by_expert(grad_received, expert_group, local_experts, capacity)
    partial_value = jnp.einsum(
        "erd,edf->erf", fwd_slots, up_local, preferred_element_type=jnp.float32
    )
    hidden = summed_on_arrival(partial_value, "shard", 2)
    active_part = jax.nn.silu(hidden).astype(jnp.bfloat16)
    active = lax.all_gather(active_part, "shard", axis=2, tiled=True)
    fwd_results = jnp.einsum(
        "erf,efd->erd", active, down_local, preferred_element_type=jnp.float32
    ).astype(jnp.bfloat16)
    fwd_returned = lax.all_to_all(
        by_source(fwd_results, expert_group, local_experts, capacity),
        "expert",
        split_axis=0,
        concat_axis=0,
        tiled=True,
    )
    layer_out = mix_rows(fwd_rows, fwd_targets, weight_fwd[0], fwd_returned)
    fwd_out = from_behind(layer_out, "section", 1)
    partial_hidden = jnp.einsum(
        "erd,edf->erf", bwd_slots, up_local, preferred_element_type=jnp.float32
    )
    partial_slope = jnp.einsum(
        "erd,efd->erf", grad_slots, down_local, preferred_element_type=jnp.float32
    )
    back_hidden, slope_in = in_one_piece((partial_hidden, partial_slope), "shard", 2, 0)
    squash = jax.nn.sigmoid(back_hidden)
    slope_part = (slope_in * squash * (1.0 + back_hidden * (1.0 - squash))).astype(jnp.bfloat16)
    slope = lax.all_gather(slope_part, "shard", axis=2, tiled=True)
    bwd_results = jnp.einsum(
        "erf,edf->erd", slope, up_local, preferred_element_type=jnp.float32
    ).astype(jnp.bfloat16)
    bwd_returned = lax.all_to_all(
        by_source(bwd_results, expert_group, local_experts, capacity),
        "expert",
        split_axis=0,
        concat_axis=0,
        tiled=True,
    )
    layer_grad = mix_rows(grad_rows, bwd_targets, weight_bwd[0], bwd_returned)
    bwd_out = from_behind(layer_grad, "section", -1)
    return (fwd_out[None], bwd_out[None])


def solution(mesh):
    in_specs = (
        P("section", "expert", "shard"),
        P("section", "expert", "shard"),
        P("section", "expert", "shard"),
        P("section", "expert", "shard", None),
        P("section", "expert", None, "shard"),
        P("section", "expert", None),
        P("section", "expert", None),
        P("section", "expert", None),
        P("section", "expert", None),
    )
    out_specs = (P("section", "expert", "shard"), P("section", "expert", "shard"))
    return jax.shard_map(
        per_device, mesh=mesh, in_specs=in_specs, out_specs=out_specs, check_vma=False
    )
```

profile of v0, /device:TPU:54, one launch (start us, length us, event | category | flops | bytes accessed | tf_op | source)
XLA Modules:
  0.0 295.4 jit_solution(17760032897972907076)
XLA Ops:
  0.6 0.9 copy.40
  1.9 0.6 reduce-window.14
  3.1 1.2 convolution_convert_fusion.2
  4.4 1.0 all_to_all.36
  5.4 15.2 %all-to-all-start = ((bf16[16,20,896]{2,1,0:T(8,128)(2,1)}), bf16[16,20,896]{2,1,0:T(8,128)(2,1)}, u32[]{:S(2)}, u32[]{:S(2)}) async-start(bf16[16,20,896]{2,1,0:T(8,128)(2,1)} %all_to_all.36), calls=%async_computation | async-start | bytes 1376256 | tf_op jit(solution)/shard_map/all_to_all | solution.py:94
  21.0 0.6 reduce-window.16
  23.0 1.2 all_to_all.42
  24.2 31.7 %all-to-all-done = bf16[16,20,896]{2,1,0:T(8,128)(2,1)} async-done(((bf16[16,20,896]{2,1,0:T(8,128)(2,1)}), bf16[16,20,896]{2,1,0:T(8,128)(2,1)}, u32[]{:S(2)}, u32[]{:S(2)}) %all-to-all-start) | async-done | bytes 573472 | tf_op jit(solution)/shard_map/all_to_all | solution.py:94
  55.9 7.2 %all-to-all-start.3 = ((bf16[16,20,1792]{2,1,0:T(8,128)(2,1)}), bf16[16,20,1792]{2,1,0:T(8,128)(2,1)S(1)}, u32[]{:S(2)}, u32[]{:S(2)}) async-start(bf16[16,20,1792]{2,1,0:T(8,128)(2,1)} %all_to_all.42), calls=%async_computation.3 | async-start | bytes 2752512 | tf_op jit(solution)/shard_map/all_to_all | solution.py:10
  63.1 3.8 %copy.53 = bf16[1024,896]{1,0:T(8,128)(2,1)} copy(bf16[1024,896]{0,1:T(8,128)(2,1)} %bitcast.127) | data formatting | bytes 3670016 | tf_op jit(solution)/shard_map/erd,edf->erf/dot_general | solution.py:107
  66.9 2.0 reshape.261
  68.9 3.6 %convolution_bitcast_fusion.2 = f32[4,1,320,256]{3,2,1,0:T(8,128)} fusion(bf16[320,896,1]{1,0,2:T(8,128)(2,1)} %reshape.261, bf16[4,256,896]{2,1,0:T(8,128)(2,1)} %bitcast.128), kind=kOutput, calls=%fused_computation.9 | convolution fusion | flops 587202560 | bytes 3719168 | tf_op jit(solution)/shard_map/erd,edf->erf/dot_general | solution.py:107
  72.6 55.1 %all-to-all-done.3 = bf16[16,20,1792]{2,1,0:T(8,128)(2,1)S(1)} async-done(((bf16[16,20,1792]{2,1,0:T(8,128)(2,1)}), bf16[16,20,1792]{2,1,0:T(8,128)(2,1)S(1)}, u32[]{:S(2)}, u32[]{:S(2)}) %all-to-all-start.3) | async-done | bytes 1146912 | tf_op jit(solution)/shard_map/all_to_all | solution.py:10
  127.7 4.3 %all-to-all-start.1 = ((f32[4,1,320,256]{3,2,1,0:T(8,128)}), f32[4,1,320,256]{3,2,1,0:T(8,128)}, u32[]{:S(2)}, u32[]{:S(2)}) async-start(f32[4,1,320,256]{3,2,1,0:T(8,128)} %convolution_bitcast_fusion.2), calls=%async_computation.1 | async-start | bytes 2621440 | tf_op jit(solution)/shard_map/all_to_all | solution.py:22
  132.0 1.1 all_to_all.44
  133.2 2.6 convolution_bitcast_fusion.1
  135.8 0.9 convolution_bitcast_fusion
  136.9 1.8 copy.52
  138.7 10.6 %all-to-all-done.1 = f32[4,1,320,256]{3,2,1,0:T(8,128)} async-done(((f32[4,1,320,256]{3,2,1,0:T(8,128)}), f32[4,1,320,256]{3,2,1,0:T(8,128)}, u32[]{:S(2)}, u32[]{:S(2)}) %all-to-all-start.1) | async-done | bytes 1310752 | tf_op jit(solution)/shard_map/all_to_all | solution.py:22
  149.3 4.6 %all-to-all-start.4 = ((f32[4,2,320,256]{3,2,1,0:T(8,128)}), f32[4,2,320,256]{3,2,1,0:T(8,128)}, u32[]{:S(2)}, u32[]{:S(2)}) async-start(f32[4,2,320,256]{3,2,1,0:T(8,128)} %copy.52), calls=%async_computation.4 | async-start | bytes 5242880 | tf_op jit(solution)/shard_map/all_to_all | solution.py:22
  153.9 1.4 reduce_sum.66
  155.4 34.1 %all_gather.6 = bf16[1,320,1024]{2,1,0:T(8,128)(2,1)S(1)} all-gather(bf16[1,320,256]{2,1,0:T(8,128)(2,1)S(1)} %fusion.17), channel_id=1, replica_groups=mesh['section'=8,'expert'=16,'shard'=4] {'shard'}, dimensions={2}, use_global_device_ids=true | all-gather | bytes 819200 | tf_op jit(solution)/shard_map/all_gather | solution.py:112
  189.5 0.8 fusion.7
  190.3 1.0 all_to_all.39
  191.3 7.4 %all-to-all-start.2 = ((bf16[16,20,896]{2,1,0:T(8,128)(2,1)}), bf16[16,20,896]{2,1,0:T(8,128)(2,1)S(1)}, u32[]{:S(2)}, u32[]{:S(2)}) async-start(bf16[16,20,896]{2,1,0:T(8,128)(2,1)} %all_to_all.39), calls=%async_computation.2 | async-start | bytes 1376256 | tf_op jit(solution)/shard_map/all_to_all | solution.py:116
  198.7 2.0 reduce_sum.72
  200.9 7.4 %all_gather.7 = bf16[1,320,1024]{2,1,0:T(8,128)(2,1)S(1)} all-gather(bf16[1,320,256]{2,1,0:T(8,128)(2,1)S(1)} %fusion.13), channel_id=1, replica_groups=mesh['section'=8,'expert'=16,'shard'=4] {'shard'}, dimensions={2}, use_global_device_ids=true | all-gather | bytes 819200 | tf_op jit(solution)/shard_map/all_gather | solution.py:134
  208.3 3.2 %fusion.4 = bf16[320,896]{1,0:T(8,128)(2,1)} fusion(bf16[1,1,896,1024]{3,2,1,0:T(8,128)(2,1)} %param.12, bf16[1,320,1024]{2,1,0:T(8,128)(2,1)S(1)} %all_gather.7), kind=kOutput, calls=%fused_computation.10 | convolution fusion | flops 587489280 | bytes 3063808 | tf_op jit(solution)/shard_map/erf,edf->erd/dot_general | solution.py:135
  211.5 2.0 all_to_all.46
  213.5 20.9 %all-to-all-done.2 = bf16[16,20,896]{2,1,0:T(8,128)(2,1)S(1)} async-done(((bf16[16,20,896]{2,1,0:T(8,128)(2,1)}), bf16[16,20,896]{2,1,0:T(8,128)(2,1)S(1)}, u32[]{:S(2)}, u32[]{:S(2)}) %all-to-all-start.2) | async-done | bytes 573472 | tf_op jit(solution)/shard_map/all_to_all | solution.py:116
  234.5 7.2 %all-to-all-start.5 = ((bf16[16,20,896]{2,1,0:T(8,128)(2,1)}), bf16[16,20,896]{2,1,0:T(8,128)(2,1)}, u32[]{:S(2)}, u32[]{:S(2)}) async-start(bf16[16,20,896]{2,1,0:T(8,128)(2,1)} %all_to_all.46), calls=%async_computation.5 | async-start | bytes 1376256 | tf_op jit(solution)/shard_map/all_to_all | solution.py:138
  242.1 0.7 copy.39
  243.1 0.7 copy.46
  243.8 0.6 pad_clamp_fusion.1
  244.4 0.6 pad_clamp_fusion
  245.1 1.3 gather_fusion
  246.4 0.5 reshape.259
  246.9 2.0 multiply_reduce_fusion.1
  249.0 0.7 add_convert_fusion.1
  249.7 2.1 collective-permute-start
  251.8 25.5 %all-to-all-done.5 = bf16[16,20,896]{2,1,0:T(8,128)(2,1)} async-done(((bf16[16,20,896]{2,1,0:T(8,128)(2,1)}), bf16[16,20,896]{2,1,0:T(8,128)(2,1)}, u32[]{:S(2)}, u32[]{:S(2)}) %all-to-all-start.5) | async-done | bytes 573472 | tf_op jit(solution)/shard_map/all_to_all | solution.py:138
  277.4 1.2 all_to_all.48
  278.6 1.2 gather_fusion.1
  280.3 1.1 multiply_reduce_fusion
  281.5 2.2 collective-permute-start.1
  283.8 9.3 %collective-permute-done.1 = bf16[128,896]{1,0:T(8,128)(2,1)S(1)} collective-permute-done((bf16[128,896]{1,0:T(8,128)(2,1)S(1)}, bf16[128,896]{1,0:T(8,128)(2,1)S(1)}, u32[]{:S(2)}, u32[]{:S(2)}) %collective-permute-start.1) | collective-permute-done | bytes 229408 | tf_op jit(solution)/shard_map/ppermute | solution.py:29
  293.1 1.6 copy.60
  294.7 0.7 copy.61
  (62 shorter events, 4.3 us)
Async XLA Ops:
  0.6 135.2 %copy-start = (bf16[1,1,1024,896]{3,2,1,0:T(8,128)(2,1)S(1)}, bf16[1,1,1024,896]{3,2,1,0:T(8,128)(2,1)}, u32[]{:S(2)}) copy-start(bf16[1,1,1024,896]{3,2,1,0:T(8,128)(2,1)} %param.13) | copy-start | bytes 5505028
  2.9 17.6 %copy-start.8 = (s32[1,128,2]{1,2,0:T(2,128)S(1)}, s32[1,128,2]{1,2,0:T(2,128)}, u32[]{:S(2)}) copy-start(s32[1,128,2]{1,2,0:T(2,128)} %param.16) | copy-start | bytes 3076
  4.4 17.9 %copy-start.4 = (bf16[1,128,896]{2,1,0:T(8,128)(2,1)S(1)}, bf16[1,128,896]{2,1,0:T(8,128)(2,1)}, u32[]{:S(2)}) copy-start(bf16[1,128,896]{2,1,0:T(8,128)(2,1)} %param.11) | copy-start | bytes 688132
  4.4 18.2 %copy-start.7 = (bf16[1,128,896]{2,1,0:T(8,128)(2,1)S(1)}, bf16[1,128,896]{2,1,0:T(8,128)(2,1)}, u32[]{:S(2)}) copy-start(bf16[1,128,896]{2,1,0:T(8,128)(2,1)} %param.10) | copy-start | bytes 688132
  5.4 50.5 %all-to-all-start = ((bf16[16,20,896]{2,1,0:T(8,128)(2,1)}), bf16[16,20,896]{2,1,0:T(8,128)(2,1)}, u32[]{:S(2)}, u32[]{:S(2)}) async-start(bf16[16,20,896]{2,1,0:T(8,128)(2,1)} %all_to_all.36), calls=%async_computation | async-start | bytes 1376256 | tf_op jit(solution)/shard_map/all_to_all | solution.py:94
  55.9 71.8 %all-to-all-start.3 = ((bf16[16,20,1792]{2,1,0:T(8,128)(2,1)}), bf16[16,20,1792]{2,1,0:T(8,128)(2,1)S(1)}, u32[]{:S(2)}, u32[]{:S(2)}) async-start(bf16[16,20,1792]{2,1,0:T(8,128)(2,1)} %all_to_all.42), calls=%async_computation.3 | async-start | bytes 2752512 | tf_op jit(solution)/shard_map/all_to_all | solution.py:10
  127.7 21.6 %all-to-all-start.1 = ((f32[4,1,320,256]{3,2,1,0:T(8,128)}), f32[4,1,320,256]{3,2,1,0:T(8,128)}, u32[]{:S(2)}, u32[]{:S(2)}) async-start(f32[4,1,320,256]{3,2,1,0:T(8,128)} %convolution_bitcast_fusion.2), calls=%async_computation.1 | async-start | bytes 2621440 | tf_op jit(solution)/shard_map/all_to_all | solution.py:22
  133.2 2.7 copy-start.2
  149.3 42.0 %all-to-all-start.4 = ((f32[4,2,320,256]{3,2,1,0:T(8,128)}), f32[4,2,320,256]{3,2,1,0:T(8,128)}, u32[]{:S(2)}, u32[]{:S(2)}) async-start(f32[4,2,320,256]{3,2,1,0:T(8,128)} %copy.52), calls=%async_computation.4 | async-start | bytes 5242880 | tf_op jit(solution)/shard_map/all_to_all | solution.py:22
  191.3 43.1 %all-to-all-start.2 = ((bf16[16,20,896]{2,1,0:T(8,128)(2,1)}), bf16[16,20,896]{2,1,0:T(8,128)(2,1)S(1)}, u32[]{:S(2)}, u32[]{:S(2)}) async-start(bf16[16,20,896]{2,1,0:T(8,128)(2,1)} %all_to_all.39), calls=%async_computation.2 | async-start | bytes 1376256 | tf_op jit(solution)/shard_map/all_to_all | solution.py:116
  211.5 30.6 %copy-start.9 = (s32[1,128,2]{1,2,0:T(2,128)S(1)}, s32[1,128,2]{1,2,0:T(2,128)}, u32[]{:S(2)}) copy-start(s32[1,128,2]{1,2,0:T(2,128)} %param.15) | copy-start | bytes 3076
  211.5 31.5 %copy-start.10 = (s32[1,128,2]{1,2,0:T(2,128)S(1)}, s32[1,128,2]{1,2,0:T(2,128)}, u32[]{:S(2)}) copy-start(s32[1,128,2]{1,2,0:T(2,128)} %param.17) | copy-start | bytes 3076
  234.5 42.9 %all-to-all-start.5 = ((bf16[16,20,896]{2,1,0:T(8,128)(2,1)}), bf16[16,20,896]{2,1,0:T(8,128)(2,1)}, u32[]{:S(2)}, u32[]{:S(2)}) async-start(bf16[16,20,896]{2,1,0:T(8,128)(2,1)} %all_to_all.46), calls=%async_computation.5 | async-start | bytes 1376256 | tf_op jit(solution)/shard_map/all_to_all | solution.py:138
  246.4 2.5 copy-start.3
  246.9 31.7 %copy-start.1 = (s32[1024]{0:T(1024)S(1)}, s32[1024]{0:T(1024)}, u32[]{:S(2)}) copy-start(s32[1024]{0:T(1024)} %pad_clamp_fusion) | copy-start | bytes 12292
  249.7 34.1 %collective-permute-start = (bf16[128,896]{1,0:T(8,128)(2,1)}, bf16[128,896]{1,0:T(8,128)(2,1)}, u32[]{:S(2)}, u32[]{:S(2)}) collective-permute-start(bf16[128,896]{1,0:T(8,128)(2,1)} %add_convert_fusion.1), channel_id=1, source_target_pairs={{0,64},{64,128},{128,192},{192,256},{256,320},{320,384},{384,448},... | collective-permute-start | bytes 688136 | tf_op jit(solution)/shard_map/ppermute | solution.py:29
  278.6 1.7 copy-start.6
  279.8 1.6 copy-start.5
  281.5 11.5 %collective-permute-start.1 = (bf16[128,896]{1,0:T(8,128)(2,1)S(1)}, bf16[128,896]{1,0:T(8,128)(2,1)S(1)}, u32[]{:S(2)}, u32[]{:S(2)}) collective-permute-start(bf16[128,896]{1,0:T(8,128)(2,1)S(1)} %add_convert_fusion), channel_id=1, source_target_pairs={{0,448},{64,0},{128,64},{192,128},{256,192},{320,256},{384,320},{4... | collective-permute-start | bytes 688136 | tf_op jit(solution)/shard_map/ppermute | solution.py:29
where the time goes:
time: 296 us; the launch traced here: 295 us
  waiting for transfers between devices  153 us (52%)
  starting transfers between devices  50.3 us (17%)
  blocking collectives  41.5 us (14%)
  local copies, waits for them, and re-layouts  25.8 us (9%)
  matrix products  13 us (4%)
  other arithmetic  10.6 us (4%)
    all_to_all x1, waiting for transfers between devices, sent_together(): lax.all_to_all(both, axis, split_axis=split_dim, concat_axis=concat_dim,...  55.1 us
    all_gather x1, blocking collectives, per_device(): active = lax.all_gather(active_part, 'shard', axis=2, tiled=True)  34.1 us
    all_to_all x1, waiting for transfers between devices, per_device(): lax.all_to_all(fwd_packed, 'expert', split_axis=0, concat_axis=0, tiled=T...  31.7 us
    all_to_all x1, waiting for transfers between devices, per_device(): lax.all_to_all(by_source(bwd_results, expert_group, local_experts, capaci...  25.5 us
    all_to_all x1, waiting for transfers between devices, per_device(): lax.all_to_all(by_source(fwd_results, expert_group, local_experts, capaci...  20.9 us
    all_to_all x1, starting transfers between devices, per_device(): lax.all_to_all(fwd_packed, 'expert', split_axis=0, concat_axis=0, tiled=T...  15.2 us
    all_to_all x2, waiting for transfers between devices, summed_on_arrival(): lax.all_to_all(tiles, axis, split_axis=0, concat_axis=0, tiled=True)  10.6 us
    ppermute x2, waiting for transfers between devices, from_behind(): return lax.ppermute(value, axis, pairs)  9.27 us
  transfers between devices with their start and end apart: 8, of which 6 were waited for; matrix products, arithmetic and copies ran while one was open for 12% of the time, Pallas kernels for 0%

commit v1 on v0

--- a/solution.py
+++ b/solution.py
@@ -2,6 +2,11 @@
 import jax.numpy as jnp
 from jax import lax
 from jax.sharding import PartitionSpec as P
+
+
+def swapped_in(x, name, along):
+    repeated = jnp.stack([x] * lax.axis_size(name))
+    return jnp.concatenate(lax.all_to_all(repeated, name, 0, 0), axis=along)
 
 
 def sent_together(arrays, axis, split_dim, concat_dim, along):
@@ -109,7 +114,7 @@
     )
     hidden = summed_on_arrival(partial_value, "shard", 2)
     active_part = jax.nn.silu(hidden).astype(jnp.bfloat16)
-    active = lax.all_gather(active_part, "shard", axis=2, tiled=True)
+    active = swapped_in(active_part, "shard", 2)
     fwd_results = jnp.einsum(
         "erf,efd->erd", active, down_local, preferred_element_type=jnp.float32
     ).astype(jnp.bfloat16)

time: 296 us -> 308 us (1.041)
  waiting for transfers between devices: 153 us -> 189 us
  blocking collectives: 41.5 us -> 6.86 us
  starting transfers between devices: 50.3 us -> 54.5 us
  other arithmetic: 10.6 us -> 14 us
    all_gather x1 -> x0, blocking collectives: 34.1 us -> none  [per_device(): active = lax.all_gather(active_part, 'shard', axis=2, tiled=True)]
    all_to_all x2, waiting for transfers between devices: 10.6 us -> 38.9 us  [summed_on_arrival(): lax.all_to_all(tiles, axis, split_axis=0, concat_axis=0, tiled=True)]
    all_to_all x1, waiting for transfers between devices: 55.1 us -> 60.3 us  [sent_together(): lax.all_to_all(both, axis, split_axis=split_dim, concat_axis=concat_dim,...]
    all_to_all x0 -> x1, starting transfers between devices: none -> 4.15 us  [swapped_in(): return jnp.concatenate(lax.all_to_all(repeated, name, 0, 0), axis=along)]
    all_to_all x0 -> x1, waiting for transfers between devices: none -> 3.58 us  [swapped_in(): return jnp.concatenate(lax.all_to_all(repeated, name, 0, 0), axis=along)]
  transfers between devices with their start and end apart: 8 -> 9, of which waited for: 6 -> 8; matrix products, arithmetic and copies ran while one was open for 12% -> 12% of each run, Pallas kernels for 0% -> 0%
where the time goes in v1:
time: 308 us; the launch traced here: 306 us
  waiting for transfers between devices  189 us (61%)
  starting transfers between devices  54.5 us (18%)
  local copies, waits for them, and re-layouts  26.8 us (9%)
  other arithmetic  14 us (5%)
  matrix products  13.9 us (5%)
  blocking collectives  6.86 us (2%)
    all_to_all x1, waiting for transfers between devices, sent_together(): lax.all_to_all(both, axis, split_axis=split_dim, concat_axis=concat_dim,...  60.3 us
    all_to_all x2, waiting for transfers between devices, summed_on_arrival(): lax.all_to_all(tiles, axis, split_axis=0, concat_axis=0, tiled=True)  38.9 us
    all_to_all x1, waiting for transfers between devices, per_device(): lax.all_to_all(fwd_packed, 'expert', split_axis=0, concat_axis=0, tiled=T...  29.9 us
    all_to_all x1, waiting for transfers between devices, per_device(): lax.all_to_all(by_source(bwd_results, expert_group, local_experts, capaci...  26.9 us
    all_to_all x1, waiting for transfers between devices, per_device(): lax.all_to_all(by_source(fwd_results, expert_group, local_experts, capaci...  20.5 us
    all_to_all x1, starting transfers between devices, per_device(): lax.all_to_all(fwd_packed, 'expert', split_axis=0, concat_axis=0, tiled=T...  15.2 us
    ppermute x2, waiting for transfers between devices, from_behind(): return lax.ppermute(value, axis, pairs)  9.27 us
    all_to_all x2, starting transfers between devices, summed_on_arrival(): lax.all_to_all(tiles, axis, split_axis=0, concat_axis=0, tiled=True)  8.08 us
  transfers between devices with their start and end apart: 9, of which 8 were waited for; matrix products, arithmetic and copies ran while one was open for 12% of the time, Pallas kernels for 0%

profile of v1, /device:TPU:54, one launch (start us, length us, event | category | flops | bytes accessed | tf_op | source)
XLA Modules:
  0.0 306.5 jit_solution(643702351757878428)
XLA Ops:
  0.6 0.9 copy.40
  3.1 1.2 convolution_convert_fusion.2
  4.4 1.0 all_to_all.39
  5.3 15.2 %all-to-all-start = ((bf16[16,20,896]{2,1,0:T(8,128)(2,1)}), bf16[16,20,896]{2,1,0:T(8,128)(2,1)S(1)}, u32[]{:S(2)}, u32[]{:S(2)}) async-start(bf16[16,20,896]{2,1,0:T(8,128)(2,1)} %all_to_all.39), calls=%async_computation | async-start | bytes 1376256 | tf_op jit(solution)/shard_map/all_to_all | solution.py:99
  21.0 3.8 %copy.54 = bf16[1024,896]{1,0:T(8,128)(2,1)} copy(bf16[1024,896]{0,1:T(8,128)(2,1)} %bitcast.117) | data formatting | bytes 3670016 | tf_op jit(solution)/shard_map/erd,edf->erf/dot_general | solution.py:112
  25.9 29.9 %all-to-all-done = bf16[16,20,896]{2,1,0:T(8,128)(2,1)S(1)} async-done(((bf16[16,20,896]{2,1,0:T(8,128)(2,1)}), bf16[16,20,896]{2,1,0:T(8,128)(2,1)S(1)}, u32[]{:S(2)}, u32[]{:S(2)}) %all-to-all-start) | async-done | bytes 573472 | tf_op jit(solution)/shard_map/all_to_all | solution.py:99
  55.9 3.4 %convolution_bitcast_fusion.2 = f32[4,1,320,256]{3,2,1,0:T(8,128)} fusion(bf16[320,896,1]{1,0,2:T(8,128)(2,1)S(1)} %reshape.256, bf16[4,256,896]{2,1,0:T(8,128)(2,1)} %bitcast.118), kind=kOutput, calls=%fused_computation.9 | convolution fusion | flops 587202560 | bytes 3719168 | tf_op jit(solution)/shard_map/erd,edf->erf/dot_general | solution.py:112
  59.3 3.5 %all-to-all-start.1 = ((f32[4,1,320,256]{3,2,1,0:T(8,128)}), f32[4,1,320,256]{3,2,1,0:T(8,128)S(1)}, u32[]{:S(2)}, u32[]{:S(2)}) async-start(f32[4,1,320,256]{3,2,1,0:T(8,128)} %convolution_bitcast_fusion.2), calls=%async_computation.1 | async-start | bytes 2621440 | tf_op jit(solution)/shard_map/all_to_all | solution.py:27
  63.1 1.2 convolution_convert_fusion
  64.3 1.2 convolution_convert_fusion.1
  65.5 1.1 pad_maximum_fusion
  66.7 2.3 all_to_all.46
  68.9 11.1 %all-to-all-done.1 = f32[4,1,320,256]{3,2,1,0:T(8,128)S(1)} async-done(((f32[4,1,320,256]{3,2,1,0:T(8,128)}), f32[4,1,320,256]{3,2,1,0:T(8,128)S(1)}, u32[]{:S(2)}, u32[]{:S(2)}) %all-to-all-start.1) | async-done | bytes 1310752 | tf_op jit(solution)/shard_map/all_to_all | solution.py:27
  80.1 1.1 copy-done.1
  81.1 7.2 %all-to-all-start.4 = ((bf16[16,20,1792]{2,1,0:T(8,128)(2,1)}), bf16[16,20,1792]{2,1,0:T(8,128)(2,1)S(1)}, u32[]{:S(2)}, u32[]{:S(2)}) async-start(bf16[16,20,1792]{2,1,0:T(8,128)(2,1)} %all_to_all.46), calls=%async_computation.4 | async-start | bytes 2752512 | tf_op jit(solution)/shard_map/all_to_all | solution.py:15
  88.4 2.2 reduce_sum.64
  90.5 1.1 multiply_convert_fusion
  91.6 60.3 %all-to-all-done.4 = bf16[16,20,1792]{2,1,0:T(8,128)(2,1)S(1)} async-done(((bf16[16,20,1792]{2,1,0:T(8,128)(2,1)}), bf16[16,20,1792]{2,1,0:T(8,128)(2,1)S(1)}, u32[]{:S(2)}, u32[]{:S(2)}) %all-to-all-start.4) | async-done | bytes 1146912 | tf_op jit(solution)/shard_map/all_to_all | solution.py:15
  151.9 0.9 stack.2
  152.8 4.2 %all-to-all-start.2 = ((bf16[4,1,320,256]{3,2,1,0:T(8,128)(2,1)}), bf16[4,1,320,256]{3,2,1,0:T(8,128)(2,1)}, u32[]{:S(2)}, u32[]{:S(2)}) async-start(bf16[4,1,320,256]{3,2,1,0:T(8,128)(2,1)} %stack.2), calls=%async_computation.2 | async-start | bytes 1310720 | tf_op jit(solution)/shard_map/all_to_all | solution.py:9
  157.0 1.1 all_to_all.48
  158.1 2.6 convolution_bitcast_fusion.1
  160.8 0.9 convolution_bitcast_fusion
  161.9 1.8 copy.53
  163.7 3.6 %all-to-all-done.2 = bf16[4,1,320,256]{3,2,1,0:T(8,128)(2,1)} async-done(((bf16[4,1,320,256]{3,2,1,0:T(8,128)(2,1)}), bf16[4,1,320,256]{3,2,1,0:T(8,128)(2,1)}, u32[]{:S(2)}, u32[]{:S(2)}) %all-to-all-start.2) | async-done | bytes 655392 | tf_op jit(solution)/shard_map/all_to_all | solution.py:9
  167.3 4.5 %all-to-all-start.5 = ((f32[4,2,320,256]{3,2,1,0:T(8,128)}), f32[4,2,320,256]{3,2,1,0:T(8,128)}, u32[]{:S(2)}, u32[]{:S(2)}) async-start(f32[4,2,320,256]{3,2,1,0:T(8,128)} %copy.53), calls=%async_computation.5 | async-start | bytes 5242880 | tf_op jit(solution)/shard_map/all_to_all | solution.py:27
  171.8 1.6 copy.46
  173.5 0.8 fusion.7
  174.4 1.0 all_to_all.43
  175.4 27.8 %all-to-all-done.5 = f32[4,2,320,256]{3,2,1,0:T(8,128)} async-done(((f32[4,2,320,256]{3,2,1,0:T(8,128)}), f32[4,2,320,256]{3,2,1,0:T(8,128)}, u32[]{:S(2)}, u32[]{:S(2)}) %all-to-all-start.5) | async-done | bytes 2621472 | tf_op jit(solution)/shard_map/all_to_all | solution.py:27
  203.2 8.0 %all-to-all-start.3 = ((bf16[16,20,896]{2,1,0:T(8,128)(2,1)}), bf16[16,20,896]{2,1,0:T(8,128)(2,1)S(1)}, u32[]{:S(2)}, u32[]{:S(2)}) async-start(bf16[16,20,896]{2,1,0:T(8,128)(2,1)} %all_to_all.43), calls=%async_computation.3 | async-start | bytes 1376256 | tf_op jit(solution)/shard_map/all_to_all | solution.py:121
  211.2 2.8 reduce_sum.69
  214.0 1.2 fusion.12
  215.2 6.9 %all_gather.3 = bf16[1,320,1024]{2,1,0:T(8,128)(2,1)S(1)} all-gather(bf16[1,320,256]{2,1,0:T(8,128)(2,1)S(1)} %fusion.12), channel_id=1, replica_groups=mesh['section'=8,'expert'=16,'shard'=4] {'shard'}, dimensions={2}, use_global_device_ids=true | all-gather | bytes 819200 | tf_op jit(solution)/shard_map/all_gather | solution.py:139
  222.1 2.4 fusion.4
  224.5 1.0 all_to_all.50
  225.5 20.5 %all-to-all-done.3 = bf16[16,20,896]{2,1,0:T(8,128)(2,1)S(1)} async-done(((bf16[16,20,896]{2,1,0:T(8,128)(2,1)}), bf16[16,20,896]{2,1,0:T(8,128)(2,1)S(1)}, u32[]{:S(2)}, u32[]{:S(2)}) %all-to-all-start.3) | async-done | bytes 573472 | tf_op jit(solution)/shard_map/all_to_all | solution.py:121
  246.0 7.4 %all-to-all-start.6 = ((bf16[16,20,896]{2,1,0:T(8,128)(2,1)}), bf16[16,20,896]{2,1,0:T(8,128)(2,1)}, u32[]{:S(2)}, u32[]{:S(2)}) async-start(bf16[16,20,896]{2,1,0:T(8,128)(2,1)} %all_to_all.50), calls=%async_computation.6 | async-start | bytes 1376256 | tf_op jit(solution)/shard_map/all_to_all | solution.py:143
  255.0 1.2 gather_fusion
  256.6 2.0 multiply_reduce_fusion.1
  259.4 2.1 collective-permute-start
  261.6 26.9 %all-to-all-done.6 = bf16[16,20,896]{2,1,0:T(8,128)(2,1)} async-done(((bf16[16,20,896]{2,1,0:T(8,128)(2,1)}), bf16[16,20,896]{2,1,0:T(8,128)(2,1)}, u32[]{:S(2)}, u32[]{:S(2)}) %all-to-all-start.6) | async-done | bytes 573472 | tf_op jit(solution)/shard_map/all_to_all | solution.py:143
  288.5 1.2 all_to_all.52
  289.7 1.2 gather_fusion.1
  291.4 1.1 multiply_reduce_fusion
  292.6 2.2 collective-permute-start.1
  294.9 9.3 %collective-permute-done.1 = bf16[128,896]{1,0:T(8,128)(2,1)S(1)} collective-permute-done((bf16[128,896]{1,0:T(8,128)(2,1)S(1)}, bf16[128,896]{1,0:T(8,128)(2,1)S(1)}, u32[]{:S(2)}, u32[]{:S(2)}) %collective-permute-start.1) | collective-permute-done | bytes 229408 | tf_op jit(solution)/shard_map/ppermute | solution.py:34
  304.1 1.6 copy.62
  (60 shorter events, 7.5 us)
Async XLA Ops:
  0.6 160.1 %copy-start = (bf16[1,1,1024,896]{3,2,1,0:T(8,128)(2,1)S(1)}, bf16[1,1,1024,896]{3,2,1,0:T(8,128)(2,1)}, u32[]{:S(2)}) copy-start(bf16[1,1,1024,896]{3,2,1,0:T(8,128)(2,1)} %param.13) | copy-start | bytes 5505028
  2.9 17.6 %copy-start.5 = (s32[1,128,2]{1,2,0:T(2,128)S(1)}, s32[1,128,2]{1,2,0:T(2,128)}, u32[]{:S(2)}) copy-start(s32[1,128,2]{1,2,0:T(2,128)} %param.16) | copy-start | bytes 3076
  5.3 50.4 %all-to-all-start = ((bf16[16,20,896]{2,1,0:T(8,128)(2,1)}), bf16[16,20,896]{2,1,0:T(8,128)(2,1)S(1)}, u32[]{:S(2)}, u32[]{:S(2)}) async-start(bf16[16,20,896]{2,1,0:T(8,128)(2,1)} %all_to_all.39), calls=%async_computation | async-start | bytes 1376256 | tf_op jit(solution)/shard_map/all_to_all | solution.py:99
  59.3 20.8 %all-to-all-start.1 = ((f32[4,1,320,256]{3,2,1,0:T(8,128)}), f32[4,1,320,256]{3,2,1,0:T(8,128)S(1)}, u32[]{:S(2)}, u32[]{:S(2)}) async-start(f32[4,1,320,256]{3,2,1,0:T(8,128)} %convolution_bitcast_fusion.2), calls=%async_computation.1 | async-start | bytes 2621440 | tf_op jit(solution)/shard_map/all_to_all | solution.py:27
  80.1 1.1 copy-start.1
  81.1 70.8 %all-to-all-start.4 = ((bf16[16,20,1792]{2,1,0:T(8,128)(2,1)}), bf16[16,20,1792]{2,1,0:T(8,128)(2,1)S(1)}, u32[]{:S(2)}, u32[]{:S(2)}) async-start(bf16[16,20,1792]{2,1,0:T(8,128)(2,1)} %all_to_all.46), calls=%async_computation.4 | async-start | bytes 2752512 | tf_op jit(solution)/shard_map/all_to_all | solution.py:15
  152.8 14.4 %all-to-all-start.2 = ((bf16[4,1,320,256]{3,2,1,0:T(8,128)(2,1)}), bf16[4,1,320,256]{3,2,1,0:T(8,128)(2,1)}, u32[]{:S(2)}, u32[]{:S(2)}) async-start(bf16[4,1,320,256]{3,2,1,0:T(8,128)(2,1)} %stack.2), calls=%async_computation.2 | async-start | bytes 1310720 | tf_op jit(solution)/shard_map/all_to_all | solution.py:9
  158.1 2.7 copy-start.2
  167.3 35.9 %all-to-all-start.5 = ((f32[4,2,320,256]{3,2,1,0:T(8,128)}), f32[4,2,320,256]{3,2,1,0:T(8,128)}, u32[]{:S(2)}, u32[]{:S(2)}) async-start(f32[4,2,320,256]{3,2,1,0:T(8,128)} %copy.53), calls=%async_computation.5 | async-start | bytes 5242880 | tf_op jit(solution)/shard_map/all_to_all | solution.py:27
  203.2 42.8 %all-to-all-start.3 = ((bf16[16,20,896]{2,1,0:T(8,128)(2,1)}), bf16[16,20,896]{2,1,0:T(8,128)(2,1)S(1)}, u32[]{:S(2)}, u32[]{:S(2)}) async-start(bf16[16,20,896]{2,1,0:T(8,128)(2,1)} %all_to_all.43), calls=%async_computation.3 | async-start | bytes 1376256 | tf_op jit(solution)/shard_map/all_to_all | solution.py:121
  224.5 29.3 %copy-start.6 = (s32[1,128,2]{1,2,0:T(2,128)S(1)}, s32[1,128,2]{1,2,0:T(2,128)}, u32[]{:S(2)}) copy-start(s32[1,128,2]{1,2,0:T(2,128)} %param.15) | copy-start | bytes 3076
  224.5 30.2 %copy-start.7 = (s32[1,128,2]{1,2,0:T(2,128)S(1)}, s32[1,128,2]{1,2,0:T(2,128)}, u32[]{:S(2)}) copy-start(s32[1,128,2]{1,2,0:T(2,128)} %param.17) | copy-start | bytes 3076
  246.0 42.5 %all-to-all-start.6 = ((bf16[16,20,896]{2,1,0:T(8,128)(2,1)}), bf16[16,20,896]{2,1,0:T(8,128)(2,1)}, u32[]{:S(2)}, u32[]{:S(2)}) async-start(bf16[16,20,896]{2,1,0:T(8,128)(2,1)} %all_to_all.50), calls=%async_computation.6 | async-start | bytes 1376256 | tf_op jit(solution)/shard_map/all_to_all | solution.py:143
  256.2 2.5 copy-start.3
  259.4 35.5 %collective-permute-start = (bf16[128,896]{1,0:T(8,128)(2,1)}, bf16[128,896]{1,0:T(8,128)(2,1)}, u32[]{:S(2)}, u32[]{:S(2)}) collective-permute-start(bf16[128,896]{1,0:T(8,128)(2,1)} %add_convert_fusion.1), channel_id=1, source_target_pairs={{0,64},{64,128},{128,192},{192,256},{256,320},{320,384},{384,448},... | collective-permute-start | bytes 688136 | tf_op jit(solution)/shard_map/ppermute | solution.py:34
  290.9 1.6 copy-start.4
  292.6 11.5 %collective-permute-start.1 = (bf16[128,896]{1,0:T(8,128)(2,1)S(1)}, bf16[128,896]{1,0:T(8,128)(2,1)S(1)}, u32[]{:S(2)}, u32[]{:S(2)}) collective-permute-start(bf16[128,896]{1,0:T(8,128)(2,1)S(1)} %add_convert_fusion), channel_id=1, source_target_pairs={{0,448},{64,0},{128,64},{192,128},{256,192},{320,256},{384,320},{4... | collective-permute-start | bytes 688136 | tf_op jit(solution)/shard_map/ppermute | solution.py:34
